TPU v7x, 256 devices: a whole 4x4x8 slice. The times are simulated.
256 devices in a mesh: dp: 8 (over z), mp: 32 (over x, y, core).
Axes of the slice: x: 4, y: 4, z: 8, core: 2. Of those that a mesh axis runs over, the one named last changes fastest.
Arguments:
- activations: bfloat16 [12288, 8192], P('dp', 'mp'), may hold values from -6 to 6
- grad_output: bfloat16 [12288, 16384], P('dp', 'mp'), may hold values from -0.0546875 to 0.0546875
- holder_index: int32 [32, 32, 1], replicated, may hold values from 0 to 31; in each aligned block of 32 rows (0 to 31, 32 to 63, ..., all dimensions but the last counted through in order) no two rows name the same one
- row_offset: int32 [32, 32], replicated, may hold values from 0 to 1
- column_offset: int32 [32, 32], replicated, may hold values from 0 to 3
- live_counts: int32 [32], replicated, may hold values from 1 to 32, as said below
Outputs:
- candidate_grads: float32 [32, 32, 128, 128], P('mp', 'dp')
Inputs may be any that keep to these rules, and one draw needn't show every extreme that they name: In each owner's 32 slots at most 1 have the same holder_index, a bound that some block reaches. Slots from live_counts[o] on are unused; some owner uses all 32 slots.
All inputs are finite; a program needn't handle non-finite values.
Results may differ from a plain program's by a relative error of at most 0.0003.
Values may be sent and summed in bfloat16 or wider, within the bound.
A program may use at most 192 MiB of HBM per device.

v0:
```python
import jax
import jax.numpy as jnp
from jax import lax
from jax.sharding import PartitionSpec as P

BLK = 128


def on_device(activations, grad_output, holder_index, row_offset, column_offset, live_counts):
    owners = lax.axis_size("mp")
    my_index = lax.axis_index("mp")
    tokens_here = activations.shape[0]
    block_size = BLK
    per_holder = activations.shape[1] // block_size
    per_owner = grad_output.shape[1] // block_size
    slot_count = row_offset.shape[1]
    holders_all = holder_index[:, :, 0]
    my_holder = lax.dynamic_index_in_dim(holders_all, my_index, 0, keepdims=False)
    my_offset = lax.dynamic_index_in_dim(row_offset, my_index, 0, keepdims=False)
    my_column = lax.dynamic_index_in_dim(column_offset, my_index, 0, keepdims=False)
    my_count = lax.dynamic_index_in_dim(live_counts, my_index, 0, keepdims=False)
    grad_panels = grad_output.reshape(tokens_here, per_owner, block_size)
    is_used = jnp.arange(slot_count, dtype=jnp.int32) < my_count
    gathered = lax.all_gather(activations, "mp", axis=1, tiled=True)
    input_panels = gathered.reshape(tokens_here, owners * per_holder, block_size)
    picked_input = jnp.take(input_panels, my_holder * per_holder + my_offset, axis=1)
    picked_grad = jnp.take(grad_panels, my_column, axis=1)
    blocks = jnp.einsum(
        "tkr,tkc->krc", picked_input, picked_grad, preferred_element_type=jnp.float32
    )
    blocks = jnp.where(is_used[:, None, None], blocks, jnp.zeros_like(blocks))
    summed = lax.psum_scatter(blocks, "dp", scatter_dimension=0, tiled=True)
    return summed[None]


def solution(mesh):
    placed = (P("dp", "mp"), P("dp", "mp"), P(), P(), P(), P())
    return jax.shard_map(
        on_device, mesh=mesh, in_specs=placed, out_specs=P("mp", "dp", None, None), check_vma=False
    )
```

profile of v0, /device:TPU:8, one launch (start us, length us, event | category | flops | bytes accessed | tf_op | source)
XLA Modules:
  0.0 218.2 jit_solution(10876988246846555151)
XLA Ops:
  6.5 0.0 all-gather.2.cloned.1.call-start
  6.5 2.3 %copy.9 = bf16[1536,256]{0,1:T(8,128)(2,1)} copy(bf16[1536,256]{1,0:T(8,128)(2,1)} %param.6) | data formatting | bytes 1572864 | tf_op args[0]
  8.9 0.0 all-gather.2.cloned.1.call-update
  8.9 0.0 reduce-scatter.2.cloned.1.call-start
  9.0 1.7 copy.11
  10.7 0.9 copy.12
  11.6 1.2 dynamic_slice.14
  12.8 0.7 fusion.15
  13.5 6.6 %gather_fusion.1 = bf16[32,1536,128]{2,1,0:T(8,128)(2,1)} fusion(bf16[1536,4,128]{2,0,1:T(8,128)(2,1)S(1)} %copy.12, s32[1024]{0:T(1024)S(1)} %pad_clamp_fusion), kind=kCustom, calls=%fused_computation.1 | custom fusion | bytes 25165952 | tf_op jit(solution)/shard_map/jit(_take)/gather | solution.py:27
  20.1 0.6 iota_compare_fusion
  20.7 0.7 fusion.14
  21.4 0.7 compare_and_fusion
  22.2 86.9 %all-gather.2.cloned.1.call-done = bf16[1536,8192]{0,1:T(8,128)(2,1)} async-done(((bf16[1536,256]{0,1:T(8,128)(2,1)}), bf16[1536,8192]{0,1:T(8,128)(2,1)}) %all-gather.2.cloned.1.call-update) | async-done | bytes 25165840 | tf_op jit(solution)/shard_map/all_gather | solution.py:24
  109.1 32.4 %copy.10 = bf16[1536,64,128]{2,0,1:T(8,128)(2,1)} copy(bf16[1536,64,128]{0,2,1:T(8,128)(2,1)} %bitcast.34) | data formatting | bytes 50331648 | tf_op jit(solution)/shard_map/reshape | solution.py:25
  141.5 14.9 %gather_fusion = bf16[32,1536,128]{2,1,0:T(8,128)(2,1)} fusion(bf16[1536,64,128]{2,0,1:T(8,128)(2,1)} %copy.10, s32[1024]{0:T(1024)S(1)} %pad_clamp_fusion.1), kind=kCustom, calls=%fused_computation | custom fusion | bytes 25165952 | tf_op jit(solution)/shard_map/jit(_take)/gather | solution.py:26
  156.4 11.9 %fusion.8 = f32[32,128,128]{2,1,0:T(8,128)} fusion(bf16[32,1536,128]{2,1,0:T(8,128)(2,1)} %gather_fusion.1, pred[32]{0:T(512)(128)(4,1)S(1)} %get-tuple-element.5, bf16[32,1536,128]{2,1,0:T(8,128)(2,1)} %gather_fusion, pred[32]{0:T(512)(128)(4,1)S(1)} %get-tuple-element.6, pred[32]{0:T(512)(128)(4,1)S(1)} %iota_compare_fusion), kind=kOutput, calls=%fused_computation.10 | convolution fusion | flops 1623719936 | bytes 27263072 | tf_op jit(solution)/shard_map/tkr,tkc->krc/dot_general | solution.py:28
  168.4 0.0 reduce-scatter.2.cloned.1.call-update
  168.4 43.0 %reduce-scatter.2.cloned.1.call-done = f32[4,128,128]{2,1,0:T(8,128)} async-done(((f32[32,128,128]{2,1,0:T(8,128)}), f32[4,128,128]{2,1,0:T(8,128)}) %reduce-scatter.2.cloned.1.call-update) | async-done | bytes 262160 | tf_op jit(solution)/shard_map/reduce_scatter | solution.py:32
  (2 shorter events, 0.0 us)
Async XLA Ops:
  6.5 102.6 %all-gather.2.cloned.1.call-start = ((), (), s32[]{:S(2)}) async-start(), calls=%async_computation.1 | async-start | bytes 25952256 | tf_op jit(solution)/shard_map/all_gather | solution.py:24
  8.9 202.5 %reduce-scatter.2.cloned.1.call-start = ((), (), s32[]{:S(2)}) async-start(), calls=%async_computation.2 | async-start | bytes 2359296 | tf_op jit(solution)/shard_map/reduce_scatter | solution.py:32
Sparse Core Ops, SparseCore 0:
  9.9 99.1 all-gather.1
  168.5 42.8 reduce-scatter.1
where the time goes:
time: 219 us; the launch traced here: 218 us
  waiting for transfers between devices  130 us (59%)
  local copies, waits for them, and re-layouts  60.1 us (27%)
  between operations  13.4 us (6%)
  matrix products  11.9 us (5%)
  other arithmetic  2.77 us (1%)
    all_gather x1, waiting for transfers between devices, on_device(): gathered = lax.all_gather(activations, 'mp', axis=1, tiled=True)  86.9 us
    reduce_scatter x1, waiting for transfers between devices, on_device(): summed = lax.psum_scatter(blocks, 'dp', scatter_dimension=0, tiled=True)  43 us
    reshape x1, local copies, waits for them, and re-layouts, on_device(): gathered.reshape(tokens_here, owners * per_holder, block_size)  32.4 us
    gather x1, local copies, waits for them, and re-layouts, on_device(): jnp.take(input_panels, my_holder * per_holder + my_offset, axis=1)  14.9 us
    dot_general x1, matrix products, on_device(): jnp.einsum('tkr,tkc->krc', picked_input, picked_grad, preferred_element_t...  11.9 us
    gather x1, local copies, waits for them, and re-layouts, on_device(): picked_grad = jnp.take(grad_panels, my_column, axis=1)  6.55 us
  transfers between devices with their start and end apart: 2, of which 2 were waited for; matrix products, arithmetic and copies ran while one was open for 6% of the time, Pallas kernels for 0%

commit v1 on v0

--- a/solution.py
+++ b/solution.py
@@ -21,7 +21,8 @@
     my_count = lax.dynamic_index_in_dim(live_counts, my_index, 0, keepdims=False)
     grad_panels = grad_output.reshape(tokens_here, per_owner, block_size)
     is_used = jnp.arange(slot_count, dtype=jnp.int32) < my_count
-    gathered = lax.all_gather(activations, "mp", axis=1, tiled=True)
+    copies = jnp.concatenate([activations] * lax.axis_size("mp"), axis=1)
+    gathered = lax.all_to_all(copies, "mp", 1, 1, tiled=True)
     input_panels = gathered.reshape(tokens_here, owners * per_holder, block_size)
     picked_input = jnp.take(input_panels, my_holder * per_holder + my_offset, axis=1)
     picked_grad = jnp.take(grad_panels, my_column, axis=1)

time: 219 us -> 620 us (2.83)
  waiting for transfers between devices: 130 us -> 443 us
  local copies, waits for them, and re-layouts: 60.1 us -> 138 us
  starting transfers between devices: 0.04 us -> 7.76 us
    all_to_all x0 -> x1, waiting for transfers between devices: none -> 398 us  [on_device(): gathered = lax.all_to_all(copies, 'mp', 1, 1, tiled=True)]
    all_gather x1 -> x0, waiting for transfers between devices: 86.9 us -> none  [on_device(): gathered = lax.all_gather(activations, 'mp', axis=1, tiled=True)]
    unnamed x2 -> x38, local copies, waits for them, and re-layouts: 4.06 us -> 49 us
    concatenate x0 -> x2, local copies, waits for them, and re-layouts: none -> 33.6 us  [on_device(): copies = jnp.concatenate([activations] * lax.axis_size('mp'), axis=1)]
    all_to_all x0 -> x1, starting transfers between devices: none -> 7.72 us  [on_device(): gathered = lax.all_to_all(copies, 'mp', 1, 1, tiled=True)]
  transfers between devices with their start and end apart: 2 -> 2, of which waited for: 2 -> 2; matrix products, arithmetic and copies ran while one was open for 6% -> 2% of each run, Pallas kernels for 0% -> 0%
where the time goes in v1:
time: 620 us; the launch traced here: 617 us
  waiting for transfers between devices  443 us (71%)
  local copies, waits for them, and re-layouts  138 us (22%)
  between operations  13.5 us (2%)
  matrix products  12 us (2%)
  starting transfers between devices  7.76 us (1%)
    all_to_all x1, waiting for transfers between devices, on_device(): gathered = lax.all_to_all(copies, 'mp', 1, 1, tiled=True)  398 us
    unnamed x38, local copies, waits for them, and re-layouts  49 us
    reduce_scatter x1, waiting for transfers between devices, on_device(): summed = lax.psum_scatter(blocks, 'dp', scatter_dimension=0, tiled=True)  45.2 us
    concatenate x2, local copies, waits for them, and re-layouts, on_device(): copies = jnp.concatenate([activations] * lax.axis_size('mp'), axis=1)  33.6 us
    reshape x1, local copies, waits for them, and re-layouts, on_device(): gathered.reshape(tokens_here, owners * per_holder, block_size)  32.5 us
    gather x1, local copies, waits for them, and re-layouts, on_device(): jnp.take(input_panels, my_holder * per_holder + my_offset, axis=1)  14.9 us
  transfers between devices with their start and end apart: 2, of which 2 were waited for; matrix products, arithmetic and copies ran while one was open for 2% of the time, Pallas kernels for 0%

profile of v1, /device:TPU:8, one launch (start us, length us, event | category | flops | bytes accessed | tf_op | source)
XLA Modules:
  0.0 617.1 jit_solution(2192591255715202992)
XLA Ops:
  6.5 2.2 constant_dynamic-update-slice_fusion.31
  8.7 2.1 constant_dynamic-update-slice_fusion.30
  10.8 2.1 constant_dynamic-update-slice_fusion.29
  12.9 2.1 constant_dynamic-update-slice_fusion.28
  15.1 2.1 constant_dynamic-update-slice_fusion.27
  17.2 2.1 constant_dynamic-update-slice_fusion.26
  19.3 2.1 constant_dynamic-update-slice_fusion.25
  21.4 2.1 constant_dynamic-update-slice_fusion.24
  23.5 2.1 constant_dynamic-update-slice_fusion.23
  25.6 2.1 constant_dynamic-update-slice_fusion.22
  27.7 2.1 constant_dynamic-update-slice_fusion.21
  29.8 2.1 constant_dynamic-update-slice_fusion.20
  31.9 2.1 constant_dynamic-update-slice_fusion.19
  34.0 2.1 constant_dynamic-update-slice_fusion.18
  36.1 2.1 constant_dynamic-update-slice_fusion.17
  38.2 2.1 constant_dynamic-update-slice_fusion.16
  40.3 0.9 constant_dynamic-update-slice_fusion.15
  41.2 0.9 constant_dynamic-update-slice_fusion.14
  42.2 1.0 constant_dynamic-update-slice_fusion.13
  43.1 1.0 constant_dynamic-update-slice_fusion.12
  44.1 1.0 constant_dynamic-update-slice_fusion.11
  45.1 1.0 constant_dynamic-update-slice_fusion.10
  46.1 0.9 constant_dynamic-update-slice_fusion.9
  47.0 0.9 constant_dynamic-update-slice_fusion.8
  48.0 1.0 constant_dynamic-update-slice_fusion.7
  48.9 1.0 constant_dynamic-update-slice_fusion.6
  49.9 1.0 constant_dynamic-update-slice_fusion.5
  50.9 0.9 constant_dynamic-update-slice_fusion.4
  51.9 1.0 constant_dynamic-update-slice_fusion.3
  52.8 1.0 constant_dynamic-update-slice_fusion.2
  53.8 1.0 constant_dynamic-update-slice_fusion.1
  54.8 1.0 constant_dynamic-update-slice_fusion
  55.8 32.6 %copy.9 = bf16[1536,8192]{0,1:T(8,128)(2,1)} copy(bf16[1536,8192]{1,0:T(8,128)(2,1)} %constant_dynamic-update-slice_fusion) | data formatting | bytes 50331648 | tf_op jit(solution)/shard_map/concatenate | solution.py:24
  88.4 7.7 %all-to-all-start = ((bf16[1536,32,256]{0,2,1:T(8,128)(2,1)}), bf16[1536,32,256]{0,2,1:T(8,128)(2,1)}, u32[]{:S(2)}, u32[]{:S(2)}) async-start(bf16[1536,32,256]{0,2,1:T(8,128)(2,1)} %bitcast.35), calls=%async_computation | async-start | bytes 50331648 | tf_op jit(solution)/shard_map/all_to_all | solution.py:25
  96.1 0.0 reduce-scatter.2.cloned.1.call-start
  96.2 0.7 copy.11
  96.9 0.9 copy.12
  97.8 0.6 dynamic_slice.14
  98.4 0.7 fusion.15
  99.1 0.7 fusion.14
  99.8 6.5 %gather_fusion.1 = bf16[32,1536,128]{2,1,0:T(8,128)(2,1)} fusion(bf16[1536,4,128]{2,0,1:T(8,128)(2,1)S(1)} %copy.12, s32[1024]{0:T(1024)S(1)} %get-tuple-element.7), kind=kCustom, calls=%fused_computation.1 | custom fusion | bytes 25165952 | tf_op jit(solution)/shard_map/jit(_take)/gather | solution.py:28
  106.3 0.6 iota_compare_fusion
  107.0 0.7 compare_and_fusion
  107.7 397.9 %all-to-all-done = bf16[1536,32,256]{0,2,1:T(8,128)(2,1)} async-done(((bf16[1536,32,256]{0,2,1:T(8,128)(2,1)}), bf16[1536,32,256]{0,2,1:T(8,128)(2,1)}, u32[]{:S(2)}, u32[]{:S(2)}) %all-to-all-start) | async-done | bytes 25165856 | tf_op jit(solution)/shard_map/all_to_all | solution.py:25
  505.6 32.5 %copy.10 = bf16[1536,64,128]{2,0,1:T(8,128)(2,1)} copy(bf16[1536,64,128]{0,2,1:T(8,128)(2,1)} %bitcast.4) | data formatting | bytes 50331648 | tf_op jit(solution)/shard_map/reshape | solution.py:26
  538.1 14.9 %gather_fusion = bf16[32,1536,128]{2,1,0:T(8,128)(2,1)} fusion(bf16[1536,64,128]{2,0,1:T(8,128)(2,1)} %copy.10, s32[1024]{0:T(1024)S(1)} %get-tuple-element.8), kind=kCustom, calls=%fused_computation | custom fusion | bytes 25165952 | tf_op jit(solution)/shard_map/jit(_take)/gather | solution.py:27
  553.0 12.0 %fusion.8 = f32[32,128,128]{2,1,0:T(8,128)} fusion(bf16[32,1536,128]{2,1,0:T(8,128)(2,1)} %gather_fusion.1, pred[32]{0:T(512)(128)(4,1)S(1)} %get-tuple-element.5, bf16[32,1536,128]{2,1,0:T(8,128)(2,1)} %gather_fusion, pred[32]{0:T(512)(128)(4,1)S(1)} %get-tuple-element.6, pred[32]{0:T(512)(128)(4,1)S(1)} %iota_compare_fusion), kind=kOutput, calls=%fused_computation.10 | convolution fusion | flops 1623719936 | bytes 27263072 | tf_op jit(solution)/shard_map/tkr,tkc->krc/dot_general | solution.py:29
  565.0 45.2 %reduce-scatter.2.cloned.1.call-done = f32[4,128,128]{2,1,0:T(8,128)} async-done(((f32[32,128,128]{2,1,0:T(8,128)}), f32[4,128,128]{2,1,0:T(8,128)}) %reduce-scatter.2.cloned.1.call-update) | async-done | bytes 262160 | tf_op jit(solution)/shard_map/reduce_scatter | solution.py:33
  (8 shorter events, 0.0 us)
Async XLA Ops:
  6.5 33.7 %copy-start = (bf16[1536,256]{1,0:T(8,128)(2,1)S(1)}, bf16[1536,256]{1,0:T(8,128)(2,1)}, u32[]{:S(2)}) copy-start(bf16[1536,256]{1,0:T(8,128)(2,1)} %param.6) | copy-start | bytes 2359300
  88.4 7.8 %copy-start.1 = (bf16[1536,512]{1,0:T(8,128)(2,1)S(1)}, bf16[1536,512]{1,0:T(8,128)(2,1)}, u32[]{:S(2)}) copy-start(bf16[1536,512]{1,0:T(8,128)(2,1)} %param.7) | copy-start | bytes 4718596
  88.4 9.4 %copy-start.2 = (s32[32]{0:T(128)S(1)}, s32[32]{0:T(128)}, u32[]{:S(2)}) copy-start(s32[32]{0:T(128)} %param.11) | copy-start | bytes 388
  88.4 417.2 %all-to-all-start = ((bf16[1536,32,256]{0,2,1:T(8,128)(2,1)}), bf16[1536,32,256]{0,2,1:T(8,128)(2,1)}, u32[]{:S(2)}, u32[]{:S(2)}) async-start(bf16[1536,32,256]{0,2,1:T(8,128)(2,1)} %bitcast.35), calls=%async_computation | async-start | bytes 50331648 | tf_op jit(solution)/shard_map/all_to_all | solution.py:25
  96.1 514.1 %reduce-scatter.2.cloned.1.call-start = ((), (), s32[]{:S(2)}) async-start(), calls=%async_computation.2 | async-start | bytes 2359296 | tf_op jit(solution)/shard_map/reduce_scatter | solution.py:33
Sparse Core Ops, SparseCore 0:
  565.1 45.0 reduce-scatter.1
